TPU v7x, 32 devices: a whole 2x2x4 slice. The times are simulated.
32 devices in a mesh: rows: 8 (over z, x), cols: 4 (over y, core).
Axes of the slice: x: 2, y: 2, z: 4, core: 2. Of those that a mesh axis runs over, the one named last changes fastest.
Arguments:
- vectors: bfloat16 [1024, 32768], P(None, 'rows'), may hold values from -0.4 to 0.4
- integrals: bfloat16 [2, 256, 32768], P(None, 'cols', 'rows'), may hold values from -8 to 72
- pivots: int32 [2, 256], replicated, may hold values from 0 to 32767, as said below
Outputs:
- new_vectors: float32 [2, 256, 32768], P(None, 'cols', 'rows')
Inputs may be any that keep to these rules, and one draw needn't show every extreme that they name: The 2 x 256 entries are distinct shell-pair rows. In each panel the rows of one index of rows (an aligned block of 4096) hold at most 64 pivots, and some block holds exactly 64.
All inputs are finite; a program needn't handle non-finite values.
Results may differ from a plain program's by a relative error of at most 0.00036.
Values may be sent and summed in bfloat16 or wider, within the bound.
No kernel may reach another device: no remote copies, remote signals or barrier semaphores. Data moves between devices by JAX's collectives and lax.ppermute only.
A program may use at most 64 MiB of HBM per device.

v0:
```python
import jax
import jax.numpy as jnp
from jax import lax
from jax.sharding import PartitionSpec as P

PW = 256
PANELS = 2


def select_matrix(row_count, targets):
    return (jnp.arange(row_count, dtype=jnp.int32)[:, None] == targets[None, :]).astype(
        jnp.bfloat16
    )


def transposed_product(left, right):
    return lax.dot_general(
        left, right, (((0,), (0,)), ((), ())), preferred_element_type=jnp.float32
    )


def solve_block(lower_factor, residual):
    return jax.scipy.linalg.solve_triangular(lower_factor, residual, lower=True)


def per_device(vectors, integrals, pivots):
    row_count = vectors.shape[1]
    block_cols = integrals.shape[1]
    owners = lax.axis_size("rows")
    owner_index = lax.axis_index("rows")
    owner_start = owner_index * row_count
    col_start = lax.axis_index("cols") * block_cols
    factors = [vectors]
    results = []
    for panel in range(PANELS):
        pivot_row = pivots[panel]
        local_targets = pivot_row - owner_start
        slot_count = 2 * PW // owners
        owner_of = pivot_row // row_count
        order = jnp.arange(PW, dtype=jnp.int32)
        earlier = (owner_of[None, :] == owner_of[:, None]) & (order[None, :] < order[:, None])
        slot_rank = jnp.sum(earlier.astype(jnp.int32), axis=1)
        mine = owner_of == owner_index
        slot_pick = (
            (slot_rank[:, None] == jnp.arange(slot_count, dtype=jnp.int32)[None, :]) & mine[:, None]
        ).astype(jnp.bfloat16)
        slot_select = jnp.dot(
            select_matrix(row_count, local_targets), slot_pick, preferred_element_type=jnp.float32
        ).astype(jnp.bfloat16)
        sending = jnp.concatenate(
            [
                jnp.dot(factor, slot_select, preferred_element_type=jnp.float32)
                for factor in factors
            ],
            axis=0,
        ).astype(jnp.bfloat16)
        targets = lax.dynamic_slice_in_dim(owner_of * slot_count + slot_rank, col_start, block_cols)
        receive_pick = select_matrix(owners * slot_count, targets)
        picked = jnp.dot(
            lax.all_gather(sending, "rows", axis=1, tiled=True),
            receive_pick,
            preferred_element_type=jnp.float32,
        ).astype(jnp.bfloat16)
        residual = integrals[panel].astype(jnp.float32)
        offset = 0
        for factor in factors:
            residual = residual - transposed_product(
                picked[offset : offset + factor.shape[0]], factor
            )
            offset = offset + factor.shape[0]
        every_pivot = select_matrix(row_count, local_targets).astype(jnp.float32)
        contribution = jnp.dot(residual, every_pivot, precision=lax.Precision.HIGHEST)
        placed = lax.dynamic_update_slice(
            jnp.zeros((PW, PW), jnp.float32), contribution, (col_start, 0)
        )
        block = lax.psum(placed, ("rows", "cols"))
        lower_factor = jnp.linalg.cholesky(0.5 * (block + block.T))
        whole = lax.all_gather(residual, "cols", axis=0, tiled=True)
        solved = solve_block(lower_factor, whole)
        fresh = lax.dynamic_slice_in_dim(solved, col_start, block_cols, 0)
        if panel + 1 < PANELS:
            factors.append(solved.astype(jnp.bfloat16))
        results.append(fresh)
    return jnp.stack(results)


def solution(mesh):
    placed = (P(None, "rows"), P(None, "cols", "rows"), P())
    return jax.shard_map(
        per_device, mesh=mesh, in_specs=placed, out_specs=P(None, "cols", "rows"), check_vma=False
    )
```

profile of v0, /device:TPU:0, one launch (start us, length us, event | category | flops | bytes accessed | tf_op | source)
XLA Modules:
  0.0 519.9 jit_solution(4560592978291593466)
XLA Ops:
  6.5 0.8 fusion.58
  7.3 0.2 convert_reduce_fusion.1
  7.5 7.5 %fusion.14 = bf16[1024,64]{0,1:T(8,128)(2,1)} fusion(bf16[1024,4096]{1,0:T(8,128)(2,1)} %param.6, s32[256]{0:T(256)S(1)} %bitcast.98, s32[256]{0:T(256)S(1)} %convert_reduce_fusion.1, pred[256]{0:T(512)(128)(4,1)S(1)} %get-tuple-element.65), kind=kOutput, calls=%fused_computation.36 | convolution fusion | flops 672497664 | bytes 8521984 | tf_op jit(solution)/shard_map/dot_general | solution.py:52
  15.2 43.0 %all-gather.5.cloned.1.call-done = bf16[1024,512]{0,1:T(8,128)(2,1)} async-done(((bf16[1024,64]{0,1:T(8,128)(2,1)}), bf16[1024,512]{0,1:T(8,128)(2,1)}) %all-gather.5.cloned.1.call-update) | async-done | bytes 1048592 | tf_op jit(solution)/shard_map/all_gather | solution.py:60
  58.2 5.9 %convolution_subtract_fusion.4 = f32[64,4096]{1,0:T(8,128)S(1)} fusion(bf16[1024,4096]{1,0:T(8,128)(2,1)} %param.6, bf16[1024,512]{0,1:T(8,128)(2,1)} %all-gather.5.cloned.1.call-done, bf16[2,64,4096]{2,1,0:T(8,128)(2,1)S(1)} %copy-done.6, s32[64]{0:T(128)S(1)} %dynamic_slice.12), kind=kOutput, calls=%fused_computation.12 | convolution fusion | flops 604602368 | bytes 11010304 | tf_op jit(solution)/shard_map/dot_general | solution.py:17
  64.1 1.7 fusion.15
  65.8 0.7 copy-done.8
  66.6 0.7 all-gather.7.cloned.1.call-update
  67.3 0.2 all-gather.9.cloned.1.call-start
  67.5 0.2 convert_reduce_fusion
  67.7 1.0 convolution_convert_fusion.1
  68.7 6.1 %fusion.13 = bf16[1024,64]{0,1:T(8,128)(2,1)S(1)} fusion(bf16[4096,64]{0,1:T(8,128)(2,1)S(1)} %convolution_convert_fusion.1, bf16[1024,4096]{1,0:T(8,128)(2,1)} %param.6), kind=kOutput, calls=%fused_computation.35 | convolution fusion | flops 536936448 | bytes 9043968 | tf_op jit(solution)/shard_map/dot_general | solution.py:52
  74.7 117.2 %all-reduce.4.cloned.1.call-done = f32[256,256]{1,0:T(8,128)} async-done(((f32[256,256]{1,0:T(8,128)}), f32[256,256]{1,0:T(8,128)}) %all-reduce.4.cloned.1.call-update) | async-done | bytes 262160 | tf_op jit(solution)/shard_map/psum | solution.py:76
  192.0 1.1 copy.9
  193.1 1.0 fusion.25
  194.1 0.1 copy.10
  194.2 11.7 %cholesky.130 = f32[128,128]{1,0:T(8,128)S(1)} custom-call(f32[128,128]{1,0:T(8,128)S(1)} %cholesky.194), custom_call_target="Cholesky" | custom-call | tf_op jit(solution)/shard_map/jit(cholesky)/cholesky | solution.py:77
  206.0 9.8 %custom-call.13 = f32[1,128,128]{1,2,0:T(8,128)S(1)} custom-call(f32[1,128,128]{2,1,0:T(8,128)S(1)} %get-tuple-element.54), custom_call_target="InvertDiagBlocksLowerTriangular" | custom-call | tf_op jit(solution)/shard_map/jit(cholesky)/cholesky | solution.py:77
  215.8 0.2 constant_dynamic-update-slice_fusion.1
  216.0 0.3 convolution_subtract_fusion.6
  216.3 11.9 %cholesky.147 = f32[128,128]{1,0:T(8,128)S(1)} custom-call(f32[128,128]{1,0:T(8,128)S(1)} %convolution_subtract_fusion.6), custom_call_target="Cholesky" | custom-call | tf_op jit(solution)/shard_map/jit(cholesky)/cholesky | solution.py:77
  228.2 0.7 compare_reduce_fusion.3
  228.9 0.7 compare_reduce_fusion.2
  231.0 4.1 while.4
  231.0 0.6 fusion.79
  231.7 1.4 bitcast_dynamic-update-slice_fusion.4
  233.1 0.6 fusion.79
  233.7 1.4 bitcast_dynamic-update-slice_fusion.4
  235.1 19.7 %custom-call.14 = f32[2,128,128]{1,2,0:T(8,128)S(1)} custom-call(f32[2,128,128]{2,1,0:T(8,128)S(1)} %get-tuple-element.21), custom_call_target="InvertDiagBlocksLowerTriangular" | custom-call | tf_op jit(solution)/shard_map/jit(_solve_triangular)/triangular_solve | solution.py:23
  254.8 3.6 fusion.5
  258.5 1.9 convolution_subtract_fusion.1
  260.4 1.9 fusion.42
  262.4 0.8 convolution_convert_fusion.5
  263.2 0.5 copy-done
  263.7 0.7 pad_maximum_fusion.2
  264.6 40.9 %all-gather.9.cloned.1.call-done = bf16[1280,512]{0,1:T(8,128)(2,1)} async-done(((bf16[1280,64]{0,1:T(8,128)(2,1)}), bf16[1280,512]{0,1:T(8,128)(2,1)}) %all-gather.9.cloned.1.call-update) | async-done | bytes 1310736 | tf_op jit(solution)/shard_map/all_gather | solution.py:60
  305.5 1.7 convolution_convert_fusion.2
  307.2 5.1 convolution_subtract_fusion.3
  312.3 0.5 convolution_subtract_fusion.2
  312.9 1.7 fusion.16
  314.6 0.7 copy-done.9
  315.3 0.4 all-gather.11.cloned.1.call-start
  315.9 0.1 fusion.20
  316.0 124.8 %all-reduce.6.cloned.1.call-done = f32[256,256]{1,0:T(8,128)} async-done(((f32[256,256]{1,0:T(8,128)}), f32[256,256]{1,0:T(8,128)}) %all-reduce.6.cloned.1.call-update) | async-done | bytes 262160 | tf_op jit(solution)/shard_map/psum | solution.py:76
  440.9 1.1 copy.11
  441.9 1.0 bitcast_add_fusion.1
  443.3 11.7 %cholesky.164 = f32[128,128]{1,0:T(8,128)S(1)} custom-call(f32[128,128]{1,0:T(8,128)S(1)} %cholesky.197), custom_call_target="Cholesky" | custom-call | tf_op jit(solution)/shard_map/jit(cholesky)/cholesky | solution.py:77
  455.0 9.8 %custom-call.15 = f32[1,128,128]{1,2,0:T(8,128)S(1)} custom-call(f32[1,128,128]{2,1,0:T(8,128)S(1)} %get-tuple-element.50), custom_call_target="InvertDiagBlocksLowerTriangular" | custom-call | tf_op jit(solution)/shard_map/jit(cholesky)/cholesky | solution.py:77
  464.9 0.2 constant_dynamic-update-slice_fusion
  465.1 0.3 convolution_subtract_fusion.5
  465.4 11.7 %cholesky.181 = f32[128,128]{1,0:T(8,128)S(1)} custom-call(f32[128,128]{1,0:T(8,128)S(1)} %convolution_subtract_fusion.5), custom_call_target="Cholesky" | custom-call | tf_op jit(solution)/shard_map/jit(cholesky)/cholesky | solution.py:77
  477.1 0.6 compare_reduce_fusion.1
  477.8 0.6 compare_reduce_fusion
  479.7 4.1 while.5
  479.9 0.6 fusion.80
  480.5 1.4 bitcast_dynamic-update-slice_fusion.5
  481.9 0.6 fusion.80
  482.5 1.4 bitcast_dynamic-update-slice_fusion.5
  483.9 19.7 %custom-call.16 = f32[2,128,128]{1,2,0:T(8,128)S(1)} custom-call(f32[2,128,128]{2,1,0:T(8,128)S(1)} %get-tuple-element.22), custom_call_target="InvertDiagBlocksLowerTriangular" | custom-call | tf_op jit(solution)/shard_map/jit(_solve_triangular)/triangular_solve | solution.py:23
  503.6 3.6 fusion.3
  507.2 1.9 convolution_subtract_fusion
  509.2 1.9 fusion.38
  511.1 0.2 fusion.18
  511.3 1.5 pad_maximum_fusion.1
  (58 shorter events, 1.3 us)
Async XLA Ops:
  6.5 51.7 %all-gather.5.cloned.1.call-start = ((), (), s32[]{:S(2)}) async-start(), calls=%async_computation | async-start | bytes 1179648 | tf_op jit(solution)/shard_map/all_gather | solution.py:60
  7.5 50.7 %copy-start.6 = (bf16[2,64,4096]{2,1,0:T(8,128)(2,1)S(1)}, bf16[2,64,4096]{2,1,0:T(8,128)(2,1)}, u32[]{:S(2)}) copy-start(bf16[2,64,4096]{2,1,0:T(8,128)(2,1)} %param.7) | copy-start | bytes 3145732
  15.0 176.9 %all-reduce.4.cloned.1.call-start = ((), (), s32[]{:S(2)}) async-start(), calls=%async_computation.1 | async-start | bytes 524288 | tf_op jit(solution)/shard_map/psum | solution.py:76
  64.1 2.5 copy-start.5
  65.8 0.7 copy-start.8
  66.5 188.3 %all-gather.7.cloned.1.call-start = ((), (), s32[]{:S(2)}) async-start(), calls=%async_computation.2 | async-start | bytes 5242880 | tf_op jit(solution)/shard_map/all_gather | solution.py:78
  67.3 238.2 %all-gather.9.cloned.1.call-start = ((), (), s32[]{:S(2)}) async-start(), calls=%async_computation.3 | async-start | bytes 1474560 | tf_op jit(solution)/shard_map/all_gather | solution.py:60
  254.8 3.7 copy-start.2
  262.4 1.3 copy-start
  263.7 43.5 %copy-start.7 = (bf16[2,64,4096]{2,1,0:T(8,128)(2,1)S(1)}, bf16[2,64,4096]{2,1,0:T(8,128)(2,1)}, u32[]{:S(2)}) copy-start(bf16[2,64,4096]{2,1,0:T(8,128)(2,1)} %param.7) | copy-start | bytes 3145732
  264.4 176.4 %all-reduce.6.cloned.1.call-start = ((), (), s32[]{:S(2)}) async-start(), calls=%async_computation.4 | async-start | bytes 524288 | tf_op jit(solution)/shard_map/psum | solution.py:76
  307.2 5.2 copy-start.1
  312.9 2.9 copy-start.4
  314.6 0.7 copy-start.9
  315.3 188.3 %all-gather.11.cloned.1.call-start = ((), (), s32[]{:S(2)}) async-start(), calls=%async_computation.5 | async-start | bytes 5242880 | tf_op jit(solution)/shard_map/all_gather | solution.py:78
  503.6 3.7 copy-start.3
Sparse Core Ops, SparseCore 0:
  15.2 42.9 all-gather.4
  66.6 125.2 all-reduce.3
  193.5 33.7 all-gather.6
  264.5 40.8 all-gather.8
  315.4 125.3 all-reduce.5
  442.3 33.6 all-gather.10
where the time goes:
time: 525 us; the launch traced here: 520 us
  waiting for transfers between devices  327 us (62%)
  other arithmetic  115 us (22%)
  matrix products  47.8 us (9%)
  between operations  16.7 us (3%)
  local copies, waits for them, and re-layouts  12.8 us (2%)
    psum x2, waiting for transfers between devices, per_device(): block = lax.psum(placed, ('rows', 'cols'))  242 us
    all_gather x2, waiting for transfers between devices, per_device(): lax.all_gather(sending, 'rows', axis=1, tiled=True)  83.9 us
    another operation x14, other arithmetic, per_device(): lower_factor = jnp.linalg.cholesky(0.5 * (block + block.T))  69.4 us
    another operation x5, other arithmetic, solve_block(): return jax.scipy.linalg.solve_triangular(lower_factor, residual, lower=True)  39.4 us
    another operation x6, matrix products, solve_block(): return jax.scipy.linalg.solve_triangular(lower_factor, residual, lower=True)  15 us
    dot_general x3, matrix products, per_device(): jnp.dot(factor, slot_select, preferred_element_type=jnp.float32)  14.4 us
    dot_general x3, matrix products, transposed_product(): lax.dot_general(left, right, (((0,), (0,)), ((), ())), preferred_element_...  11.5 us
  transfers between devices with their start and end apart: 6, of which 4 were waited for; matrix products, arithmetic and copies ran while one was open for 25% of the time, Pallas kernels for 0%

commit v1 on v0

--- a/solution.py
+++ b/solution.py
@@ -73,7 +73,7 @@
         placed = lax.dynamic_update_slice(
             jnp.zeros((PW, PW), jnp.float32), contribution, (col_start, 0)
         )
-        block = lax.psum(placed, ("rows", "cols"))
+        block = lax.psum(lax.psum(placed, "rows"), "cols")
         lower_factor = jnp.linalg.cholesky(0.5 * (block + block.T))
         whole = lax.all_gather(residual, "cols", axis=0, tiled=True)
         solved = solve_block(lower_factor, whole)

time: 525 us -> 483 us (0.920)
  waiting for transfers between devices: 327 us -> 284 us
    psum x2 -> x4, waiting for transfers between devices: 242 us -> 199 us  [per_device(): block = lax.psum(lax.psum(placed, 'rows'), 'cols')]
  transfers between devices with their start and end apart: 6 -> 8, of which waited for: 4 -> 6; matrix products, arithmetic and copies ran while one was open for 25% -> 27% of each run, Pallas kernels for 0% -> 0%
where the time goes in v1:
time: 483 us; the launch traced here: 477 us
  waiting for transfers between devices  284 us (59%)
  other arithmetic  115 us (24%)
  matrix products  47.8 us (10%)
  between operations  16.7 us (3%)
  local copies, waits for them, and re-layouts  12.8 us (3%)
    psum x4, waiting for transfers between devices, per_device(): block = lax.psum(lax.psum(placed, 'rows'), 'cols')  199 us
    all_gather x2, waiting for transfers between devices, per_device(): lax.all_gather(sending, 'rows', axis=1, tiled=True)  84.8 us
    another operation x14, other arithmetic, per_device(): lower_factor = jnp.linalg.cholesky(0.5 * (block + block.T))  69.5 us
    another operation x5, other arithmetic, solve_block(): return jax.scipy.linalg.solve_triangular(lower_factor, residual, lower=True)  39.4 us
    another operation x6, matrix products, solve_block(): return jax.scipy.linalg.solve_triangular(lower_factor, residual, lower=True)  15 us
    dot_general x3, matrix products, per_device(): jnp.dot(factor, slot_select, preferred_element_type=jnp.float32)  14.3 us
    dot_general x3, matrix products, transposed_product(): lax.dot_general(left, right, (((0,), (0,)), ((), ())), preferred_element_...  11.5 us
  transfers between devices with their start and end apart: 8, of which 6 were waited for; matrix products, arithmetic and copies ran while one was open for 27% of the time, Pallas kernels for 0%

profile of v1, /device:TPU:0, one launch (start us, length us, event | category | flops | bytes accessed | tf_op | source)
XLA Modules:
  0.0 477.5 jit_solution(16614069924963970774)
XLA Ops:
  6.5 0.8 fusion.58
  7.3 0.2 convert_reduce_fusion.1
  7.5 7.5 %fusion.14 = bf16[1024,64]{0,1:T(8,128)(2,1)} fusion(bf16[1024,4096]{1,0:T(8,128)(2,1)} %param.6, s32[256]{0:T(256)S(1)} %bitcast.98, s32[256]{0:T(256)S(1)} %convert_reduce_fusion.1, pred[256]{0:T(512)(128)(4,1)S(1)} %get-tuple-element.65), kind=kOutput, calls=%fused_computation.36 | convolution fusion | flops 672497664 | bytes 8521984 | tf_op jit(solution)/shard_map/dot_general | solution.py:52
  15.2 43.0 %all-gather.5.cloned.1.call-done = bf16[1024,512]{0,1:T(8,128)(2,1)} async-done(((bf16[1024,64]{0,1:T(8,128)(2,1)}), bf16[1024,512]{0,1:T(8,128)(2,1)}) %all-gather.5.cloned.1.call-update) | async-done | bytes 1048592 | tf_op jit(solution)/shard_map/all_gather | solution.py:60
  58.2 5.9 %convolution_subtract_fusion.4 = f32[64,4096]{1,0:T(8,128)S(1)} fusion(bf16[1024,4096]{1,0:T(8,128)(2,1)} %param.6, bf16[1024,512]{0,1:T(8,128)(2,1)} %all-gather.5.cloned.1.call-done, bf16[2,64,4096]{2,1,0:T(8,128)(2,1)S(1)} %copy-done.6, s32[64]{0:T(128)S(1)} %dynamic_slice.12), kind=kOutput, calls=%fused_computation.12 | convolution fusion | flops 604602368 | bytes 11010304 | tf_op jit(solution)/shard_map/dot_general | solution.py:17
  64.1 1.7 fusion.15
  65.8 0.7 copy-done.8
  66.5 69.9 %all-reduce.6.cloned.1.call-done = f32[256,256]{1,0:T(8,128)} async-done(((f32[256,256]{1,0:T(8,128)}), f32[256,256]{1,0:T(8,128)}) %all-reduce.6.cloned.1.call-update) | async-done | bytes 262160 | tf_op jit(solution)/shard_map/psum | solution.py:76
  136.5 0.5 all-gather.7.cloned.1.call-update
  137.0 0.2 all-gather.9.cloned.1.call-start
  137.4 1.0 convolution_convert_fusion.1
  138.4 6.0 %fusion.13 = bf16[1024,64]{0,1:T(8,128)(2,1)S(1)} fusion(bf16[4096,64]{0,1:T(8,128)(2,1)S(1)} %convolution_convert_fusion.1, bf16[1024,4096]{1,0:T(8,128)(2,1)} %param.6), kind=kOutput, calls=%fused_computation.35 | convolution fusion | flops 536936448 | bytes 9043968 | tf_op jit(solution)/shard_map/dot_general | solution.py:52
  144.4 25.9 %all-reduce.8.cloned.1.call-done = f32[256,256]{1,0:T(8,128)} async-done(((f32[256,256]{1,0:T(8,128)}), f32[256,256]{1,0:T(8,128)}) %all-reduce.8.cloned.1.call-update) | async-done | bytes 262160 | tf_op jit(solution)/shard_map/psum | solution.py:76
  170.3 1.1 copy.9
  171.4 1.0 fusion.25
  172.6 11.7 %cholesky.130 = f32[128,128]{1,0:T(8,128)S(1)} custom-call(f32[128,128]{1,0:T(8,128)S(1)} %cholesky.194), custom_call_target="Cholesky" | custom-call | tf_op jit(solution)/shard_map/jit(cholesky)/cholesky | solution.py:77
  184.3 9.8 %custom-call.13 = f32[1,128,128]{1,2,0:T(8,128)S(1)} custom-call(f32[1,128,128]{2,1,0:T(8,128)S(1)} %get-tuple-element.54), custom_call_target="InvertDiagBlocksLowerTriangular" | custom-call | tf_op jit(solution)/shard_map/jit(cholesky)/cholesky | solution.py:77
  194.2 0.2 constant_dynamic-update-slice_fusion.1
  194.4 0.3 convolution_subtract_fusion.6
  194.7 11.9 %cholesky.147 = f32[128,128]{1,0:T(8,128)S(1)} custom-call(f32[128,128]{1,0:T(8,128)S(1)} %convolution_subtract_fusion.6), custom_call_target="Cholesky" | custom-call | tf_op jit(solution)/shard_map/jit(cholesky)/cholesky | solution.py:77
  206.6 0.7 compare_reduce_fusion.3
  207.3 0.7 compare_reduce_fusion.2
  209.4 4.1 while.4
  209.4 0.6 fusion.79
  210.1 1.4 bitcast_dynamic-update-slice_fusion.4
  211.5 0.6 fusion.79
  212.1 1.4 bitcast_dynamic-update-slice_fusion.4
  213.5 19.7 %custom-call.14 = f32[2,128,128]{1,2,0:T(8,128)S(1)} custom-call(f32[2,128,128]{2,1,0:T(8,128)S(1)} %get-tuple-element.21), custom_call_target="InvertDiagBlocksLowerTriangular" | custom-call | tf_op jit(solution)/shard_map/jit(_solve_triangular)/triangular_solve | solution.py:23
  233.2 3.6 fusion.5
  236.9 1.9 convolution_subtract_fusion.1
  238.8 1.9 fusion.42
  240.8 0.8 convolution_convert_fusion.5
  241.6 0.5 copy-done
  242.1 0.7 pad_maximum_fusion.2
  243.0 41.8 %all-gather.9.cloned.1.call-done = bf16[1280,512]{0,1:T(8,128)(2,1)} async-done(((bf16[1280,64]{0,1:T(8,128)(2,1)}), bf16[1280,512]{0,1:T(8,128)(2,1)}) %all-gather.9.cloned.1.call-update) | async-done | bytes 1310736 | tf_op jit(solution)/shard_map/all_gather | solution.py:60
  284.8 1.7 convolution_convert_fusion.2
  286.5 5.1 %convolution_subtract_fusion.3 = f32[64,4096]{1,0:T(8,128)S(1)} fusion(bf16[1024,4096]{1,0:T(8,128)(2,1)} %param.6, bf16[2,64,4096]{2,1,0:T(8,128)(2,1)S(1)} %copy-done.7, bf16[1280,64]{0,1:T(8,128)(2,1)S(1)} %convolution_convert_fusion.2), kind=kOutput, calls=%fused_computation.11 | convolution fusion | flops 537395200 | bytes 10092544 | tf_op jit(solution)/shard_map/dot_general | solution.py:17
  291.7 0.5 convolution_subtract_fusion.2
  292.2 1.7 fusion.16
  293.9 0.7 copy-done.9
  294.7 69.9 %all-reduce.10.cloned.1.call-done = f32[256,256]{1,0:T(8,128)} async-done(((f32[256,256]{1,0:T(8,128)}), f32[256,256]{1,0:T(8,128)}) %all-reduce.10.cloned.1.call-update) | async-done | bytes 262160 | tf_op jit(solution)/shard_map/psum | solution.py:76
  364.6 0.4 all-gather.11.cloned.1.call-start
  365.1 0.3 all-gather.11.cloned.1.call-update
  365.5 32.9 %all-reduce.12.cloned.1.call-done = f32[256,256]{1,0:T(8,128)} async-done(((f32[256,256]{1,0:T(8,128)}), f32[256,256]{1,0:T(8,128)}) %all-reduce.12.cloned.1.call-update) | async-done | bytes 262160 | tf_op jit(solution)/shard_map/psum | solution.py:76
  398.4 1.1 copy.11
  399.5 1.0 bitcast_add_fusion.1
  400.9 11.7 %cholesky.164 = f32[128,128]{1,0:T(8,128)S(1)} custom-call(f32[128,128]{1,0:T(8,128)S(1)} %cholesky.197), custom_call_target="Cholesky" | custom-call | tf_op jit(solution)/shard_map/jit(cholesky)/cholesky | solution.py:77
  412.6 9.8 %custom-call.15 = f32[1,128,128]{1,2,0:T(8,128)S(1)} custom-call(f32[1,128,128]{2,1,0:T(8,128)S(1)} %get-tuple-element.50), custom_call_target="InvertDiagBlocksLowerTriangular" | custom-call | tf_op jit(solution)/shard_map/jit(cholesky)/cholesky | solution.py:77
  422.5 0.2 constant_dynamic-update-slice_fusion
  422.7 0.3 convolution_subtract_fusion.5
  422.9 11.7 %cholesky.181 = f32[128,128]{1,0:T(8,128)S(1)} custom-call(f32[128,128]{1,0:T(8,128)S(1)} %convolution_subtract_fusion.5), custom_call_target="Cholesky" | custom-call | tf_op jit(solution)/shard_map/jit(cholesky)/cholesky | solution.py:77
  434.7 0.6 compare_reduce_fusion.1
  435.3 0.6 compare_reduce_fusion
  437.3 4.1 while.5
  437.5 0.6 fusion.80
  438.1 1.4 bitcast_dynamic-update-slice_fusion.5
  439.5 0.6 fusion.80
  440.1 1.4 bitcast_dynamic-update-slice_fusion.5
  441.4 19.7 %custom-call.16 = f32[2,128,128]{1,2,0:T(8,128)S(1)} custom-call(f32[2,128,128]{2,1,0:T(8,128)S(1)} %get-tuple-element.22), custom_call_target="InvertDiagBlocksLowerTriangular" | custom-call | tf_op jit(solution)/shard_map/jit(_solve_triangular)/triangular_solve | solution.py:23
  461.2 3.6 fusion.3
  464.8 1.9 convolution_subtract_fusion
  466.7 1.9 fusion.38
  468.7 0.2 fusion.18
  468.9 1.5 pad_maximum_fusion.1
  (64 shorter events, 1.8 us)
Async XLA Ops:
  6.5 51.7 %all-gather.5.cloned.1.call-start = ((), (), s32[]{:S(2)}) async-start(), calls=%async_computation | async-start | bytes 1179648 | tf_op jit(solution)/shard_map/all_gather | solution.py:60
  7.5 50.7 %copy-start.6 = (bf16[2,64,4096]{2,1,0:T(8,128)(2,1)S(1)}, bf16[2,64,4096]{2,1,0:T(8,128)(2,1)}, u32[]{:S(2)}) copy-start(bf16[2,64,4096]{2,1,0:T(8,128)(2,1)} %param.7) | copy-start | bytes 3145732
  15.0 121.4 %all-reduce.6.cloned.1.call-start = ((), (), s32[]{:S(2)}) async-start(), calls=%async_computation.1 | async-start | bytes 524288 | tf_op jit(solution)/shard_map/psum | solution.py:76
  64.1 72.4 %copy-start.5 = (f32[64,4096]{1,0:T(8,128)}, f32[64,4096]{1,0:T(8,128)S(1)}, u32[]{:S(2)}) copy-start(f32[64,4096]{1,0:T(8,128)S(1)} %convolution_subtract_fusion.4) | copy-start | bytes 3145732
  65.8 0.7 copy-start.8
  66.5 103.8 %all-reduce.8.cloned.1.call-start = ((), (), s32[]{:S(2)}) async-start(), calls=%async_computation.2 | async-start | bytes 524288 | tf_op jit(solution)/shard_map/psum | solution.py:76
  136.4 96.8 %all-gather.7.cloned.1.call-start = ((), (), s32[]{:S(2)}) async-start(), calls=%async_computation.3 | async-start | bytes 5242880 | tf_op jit(solution)/shard_map/all_gather | solution.py:78
  137.0 147.8 %all-gather.9.cloned.1.call-start = ((), (), s32[]{:S(2)}) async-start(), calls=%async_computation.4 | async-start | bytes 1474560 | tf_op jit(solution)/shard_map/all_gather | solution.py:60
  233.2 3.7 copy-start.2
  240.8 1.3 copy-start
  242.1 44.4 %copy-start.7 = (bf16[2,64,4096]{2,1,0:T(8,128)(2,1)S(1)}, bf16[2,64,4096]{2,1,0:T(8,128)(2,1)}, u32[]{:S(2)}) copy-start(bf16[2,64,4096]{2,1,0:T(8,128)(2,1)} %param.7) | copy-start | bytes 3145732
  242.8 121.8 %all-reduce.10.cloned.1.call-start = ((), (), s32[]{:S(2)}) async-start(), calls=%async_computation.5 | async-start | bytes 524288 | tf_op jit(solution)/shard_map/psum | solution.py:76
  286.5 5.2 %copy-start.1 = (f32[128,4096]{1,0:T(8,128)S(1)}, f32[128,4096]{1,0:T(8,128)}, u32[]{:S(2)}) copy-start(f32[128,4096]{1,0:T(8,128)} %copy-done) | copy-start | bytes 6291460
  292.2 72.9 %copy-start.4 = (f32[64,4096]{1,0:T(8,128)}, f32[64,4096]{1,0:T(8,128)S(1)}, u32[]{:S(2)}) copy-start(f32[64,4096]{1,0:T(8,128)S(1)} %convolution_subtract_fusion.2) | copy-start | bytes 3145732
  293.9 0.7 copy-start.9
  294.6 103.8 %all-reduce.12.cloned.1.call-start = ((), (), s32[]{:S(2)}) async-start(), calls=%async_computation.6 | async-start | bytes 524288 | tf_op jit(solution)/shard_map/psum | solution.py:76
  364.6 96.5 %all-gather.11.cloned.1.call-start = ((), (), s32[]{:S(2)}) async-start(), calls=%async_computation.7 | async-start | bytes 5242880 | tf_op jit(solution)/shard_map/all_gather | solution.py:78
  461.1 3.7 copy-start.3
Sparse Core Ops, SparseCore 0:
  15.2 42.9 all-gather.4
  66.6 69.7 all-reduce.5
  138.7 31.5 all-reduce.7
  171.7 34.5 all-gather.6
  242.9 41.8 all-gather.8
  294.7 69.8 all-reduce.9
  366.9 31.4 all-reduce.11
  400.0 34.4 all-gather.10
